TPU v7x, 32 devices: a whole 2x2x4 slice. The times are simulated.
32 devices in a mesh: fsdp: 4 (over y, core), context: 4 (over z), tensor: 2 (over x).
Axes of the slice: x: 2, y: 2, z: 4, core: 2. Of those that a mesh axis runs over, the one named last changes fastest.
Arguments:
- hidden_in: float32 [4, 512, 2560], P('fsdp', 'context'), may hold values from -6 to 6
- cotangent: float32 [4, 512, 2560], P('fsdp', 'context'), may hold values from -6 to 6
- segment_ids: int32 [4, 512], P('fsdp', 'context'), may hold values from 0 to 3, as said below
- positions: int32 [4, 512], P('fsdp', 'context'), may hold values from 0 to 511, as said below
- attn_scale: float32 [2560], P(('fsdp', 'context')), may hold values from -0.5 to 0.5
- query_weight: float32 [2560, 2560], P(('fsdp', 'context'), 'tensor')
- keyval_weight: float32 [2560, 512], P(('fsdp', 'context'))
- output_weight: float32 [2560, 2560], P('tensor', ('fsdp', 'context')), may hold values from -0.5 to 0.5
- mlp_scale: float32 [2560], P(('fsdp', 'context')), may hold values from -0.5 to 0.5
- gate_weight: float32 [2560, 7680], P(('fsdp', 'context'), 'tensor'), may hold values from -0.125 to 0.125
- up_weight: float32 [2560, 7680], P(('fsdp', 'context'), 'tensor'), may hold values from -0.125 to 0.125
- down_weight: float32 [7680, 2560], P('tensor', ('fsdp', 'context')), may hold values from -0.0625 to 0.0625
- first_attn_scale: float32 [2560], P(('fsdp', 'context')), may hold values from -40 to 40
- first_query_weight: float32 [2560, 2560], P(('fsdp', 'context'), 'tensor'), may hold values from -16 to 16
- first_keyval_weight: float32 [2560, 512], P(('fsdp', 'context')), may hold values from -80 to 80
- first_output_weight: float32 [2560, 2560], P('tensor', ('fsdp', 'context')), may hold values from -4 to 4
- first_mlp_scale: float32 [2560], P(('fsdp', 'context')), may hold values from -20 to 20
- first_gate_weight: float32 [2560, 7680], P(('fsdp', 'context'), 'tensor'), may hold values from -16 to 16
- first_up_weight: float32 [2560, 7680], P(('fsdp', 'context'), 'tensor'), may hold values from -16 to 16
- first_down_weight: float32 [7680, 2560], P('tensor', ('fsdp', 'context')), may hold values from -24 to 24
- second_attn_scale: float32 [2560], P(('fsdp', 'context')), may hold values from 0.6144 to 6.144
- second_query_weight: float32 [2560, 2560], P(('fsdp', 'context'), 'tensor'), may hold values from 0.1024 to 1.024
- second_keyval_weight: float32 [2560, 512], P(('fsdp', 'context')), may hold values from 2.4576 to 24.576
- second_output_weight: float32 [2560, 2560], P('tensor', ('fsdp', 'context')), may hold values from 0.006 to 0.06
- second_mlp_scale: float32 [2560], P(('fsdp', 'context')), may hold values from 0.2048 to 2.048
- second_gate_weight: float32 [2560, 7680], P(('fsdp', 'context'), 'tensor'), may hold values from 0.1024 to 1.024
- second_up_weight: float32 [2560, 7680], P(('fsdp', 'context'), 'tensor'), may hold values from 0.1024 to 1.024
- second_down_weight: float32 [7680, 2560], P('tensor', ('fsdp', 'context')), may hold values from 0.2048 to 2.048
Outputs:
- block_output: float32 [4, 512, 2560], P('fsdp', 'context')
- input_grad: float32 [4, 512, 2560], P('fsdp', 'context')
- grad_attn_scale: float32 [2560], P(('fsdp', 'context'))
- grad_query_weight: float32 [2560, 2560], P(('fsdp', 'context'), 'tensor')
- grad_keyval_weight: float32 [2560, 512], P(('fsdp', 'context'))
- grad_output_weight: float32 [2560, 2560], P('tensor', ('fsdp', 'context'))
- grad_mlp_scale: float32 [2560], P(('fsdp', 'context'))
- grad_gate_weight: float32 [2560, 7680], P(('fsdp', 'context'), 'tensor')
- grad_up_weight: float32 [2560, 7680], P(('fsdp', 'context'), 'tensor')
- grad_down_weight: float32 [7680, 2560], P('tensor', ('fsdp', 'context'))
- new_attn_scale: float32 [2560], P(('fsdp', 'context'))
- new_query_weight: float32 [2560, 2560], P(('fsdp', 'context'), 'tensor')
- new_keyval_weight: float32 [2560, 512], P(('fsdp', 'context'))
- new_output_weight: float32 [2560, 2560], P('tensor', ('fsdp', 'context'))
- new_mlp_scale: float32 [2560], P(('fsdp', 'context'))
- new_gate_weight: float32 [2560, 7680], P(('fsdp', 'context'), 'tensor')
- new_up_weight: float32 [2560, 7680], P(('fsdp', 'context'), 'tensor')
- new_down_weight: float32 [7680, 2560], P('tensor', ('fsdp', 'context'))
- new_first_attn_scale: float32 [2560], P(('fsdp', 'context'))
- new_first_query_weight: float32 [2560, 2560], P(('fsdp', 'context'), 'tensor')
- new_first_keyval_weight: float32 [2560, 512], P(('fsdp', 'context'))
- new_first_output_weight: float32 [2560, 2560], P('tensor', ('fsdp', 'context'))
- new_first_mlp_scale: float32 [2560], P(('fsdp', 'context'))
- new_first_gate_weight: float32 [2560, 7680], P(('fsdp', 'context'), 'tensor')
- new_first_up_weight: float32 [2560, 7680], P(('fsdp', 'context'), 'tensor')
- new_first_down_weight: float32 [7680, 2560], P('tensor', ('fsdp', 'context'))
- new_second_attn_scale: float32 [2560], P(('fsdp', 'context'))
- new_second_query_weight: float32 [2560, 2560], P(('fsdp', 'context'), 'tensor')
- new_second_keyval_weight: float32 [2560, 512], P(('fsdp', 'context'))
- new_second_output_weight: float32 [2560, 2560], P('tensor', ('fsdp', 'context'))
- new_second_mlp_scale: float32 [2560], P(('fsdp', 'context'))
- new_second_gate_weight: float32 [2560, 7680], P(('fsdp', 'context'), 'tensor')
- new_second_up_weight: float32 [2560, 7680], P(('fsdp', 'context'), 'tensor')
- new_second_down_weight: float32 [7680, 2560], P('tensor', ('fsdp', 'context'))
Inputs may be any that keep to these rules, and one draw needn't show every extreme that they name: segment_ids start at 0 and never fall along a sequence; a document is a run of equal values; the first sequence is one document, every other sequence holds four. positions count the tokens from the first token of the token's document, which has 0.
All inputs are finite; a program needn't handle non-finite values.
Results may differ from a plain program's by a relative error of at most 0.014.
Values may be sent and summed in bfloat16 or wider, within the bound.
A program may use at most 448 MiB of HBM per device.

v0:
```python
import jax
import jax.numpy as jnp
from jax import lax
from jax.sharding import PartitionSpec as P

HD = 256
norm_eps = 1e-06
beta_one = 0.9
beta_two = 0.999
adam_eps = 1e-08
learn_rate = 0.03
decay_rate = 0.1
adam_step = 4.0
rope_base = 10000.0
masked_value = -1e30
single = jnp.float32
half_type = jnp.bfloat16


def gelu_tanh(values):
    return jax.nn.gelu(values, approximate=True)


def rope_tables(positions):
    half = HD // 2
    freq = rope_base ** (-2.0 * jnp.arange(half).astype(jnp.float32) / HD)
    angle = positions.astype(jnp.float32)[..., None] * freq
    return (jnp.cos(angle), jnp.sin(angle))


def rotate(values, cosine, sine):
    half = values.shape[-1] // 2
    first = values[..., :half]
    second = values[..., half:]
    return jnp.concatenate(
        [first * cosine - second * sine, second * cosine + first * sine], axis=-1
    )


def unrotate(values, cosine, sine):
    half = values.shape[-1] // 2
    first = values[..., :half]
    second = values[..., half:]
    return jnp.concatenate(
        [first * cosine + second * sine, second * cosine - first * sine], axis=-1
    )


def rms_forward(values, scale):
    inverse = lax.rsqrt(jnp.mean(values * values, axis=-1, keepdims=True) + norm_eps)
    normed = values * inverse
    return (normed, inverse, (normed * (1.0 + scale)).astype(jnp.bfloat16))


def rms_backward(dnorm, normed, inverse, scale):
    dnormed = dnorm * (1.0 + scale)
    dvalues = inverse * (dnormed - normed * jnp.mean(dnormed * normed, axis=-1, keepdims=True))
    return (dvalues, dnorm * normed)


def adamw(weight, grad, first, second):
    first_new = beta_one * first + (1.0 - beta_one) * grad
    second_new = beta_two * second + (1.0 - beta_two) * grad * grad
    fix_one = 1.0 - beta_one**adam_step
    fix_two = 1.0 - beta_two**adam_step
    update = first_new / fix_one / (jnp.sqrt(second_new / fix_two) + adam_eps)
    return (weight - learn_rate * (update + decay_rate * weight), first_new, second_new)


def dot(a, b, dims):
    return lax.dot_general(a, b, (dims, ((), ())), preferred_element_type=single)


def small_gather(attn_scale, mlp_scale, segment_ids):
    scales = jnp.stack([attn_scale, mlp_scale]).astype(half_type)
    scales = lax.all_gather(scales, ("fsdp", "context"), axis=1, tiled=True).astype(single)
    seg_all = lax.all_gather(segment_ids, "context", axis=1, tiled=True)
    return (scales[0], scales[1], seg_all)


def gather_rows(block):
    return lax.all_gather(block, ("fsdp", "context"), axis=0, tiled=True)


def prepare_slice(block):
    rows, columns = block.shape
    ctx = lax.axis_size("context")
    parts = block.reshape(rows, ctx, columns // ctx).transpose(1, 0, 2)
    parts = lax.all_to_all(parts, "context", split_axis=0, concat_axis=0, tiled=True)
    full = lax.all_gather(parts, "fsdp", axis=0, tiled=True)
    return full.reshape(-1, columns // ctx)


def gather_tokens(block):
    return lax.all_gather(block, ("context", "tensor"), axis=0, tiled=True)


def scatter_tokens(part):
    return lax.psum_scatter(
        part.astype(half_type), ("context", "tensor"), scatter_dimension=0, tiled=True
    ).astype(single)


def scatter_rows(part):
    return lax.psum_scatter(
        part.astype(half_type), ("fsdp", "context"), scatter_dimension=0, tiled=True
    ).astype(single)


def return_slice(part):
    full, columns = part.shape
    ctx = lax.axis_size("context")
    fs = lax.axis_size("fsdp")
    rows = full // (ctx * fs)
    parts = part.astype(half_type).reshape(fs * ctx, rows, columns)
    parts = lax.psum_scatter(parts, "fsdp", scatter_dimension=0, tiled=True)
    parts = lax.all_to_all(parts, "context", split_axis=0, concat_axis=0, tiled=True)
    return parts.transpose(1, 0, 2).reshape(rows, ctx * columns).astype(single)


def on_device(
    hidden_in,
    cotangent,
    segment_ids,
    positions,
    attn_scale,
    query_weight,
    keyval_weight,
    output_weight,
    mlp_scale,
    gate_weight,
    up_weight,
    down_weight,
    first_attn_scale,
    first_query_weight,
    first_keyval_weight,
    first_output_weight,
    first_mlp_scale,
    first_gate_weight,
    first_up_weight,
    first_down_weight,
    second_attn_scale,
    second_query_weight,
    second_keyval_weight,
    second_output_weight,
    second_mlp_scale,
    second_gate_weight,
    second_up_weight,
    second_down_weight,
):
    ten = lax.axis_size("tensor")
    x = lax.axis_index("tensor")
    context_index = lax.axis_index("context")
    block, width = hidden_in.shape[1:]
    half_rows = block // ten
    heads_here = query_weight.shape[1] // HD
    heads_width = heads_here * HD
    hidden = hidden_in[0]
    cot = cotangent[0]
    hidden_half = lax.dynamic_slice_in_dim(hidden, x * half_rows, half_rows, 0)
    cot_half = lax.dynamic_slice_in_dim(cot, x * half_rows, half_rows, 0)
    scale_one, scale_two, seg_all = small_gather(attn_scale, mlp_scale, segment_ids)
    query_full = gather_rows(query_weight.astype(half_type))
    keyval_full = gather_rows(keyval_weight.astype(half_type))
    output_full = gather_rows(output_weight.astype(half_type).T)
    gate_slice = prepare_slice(gate_weight.astype(half_type))
    up_slice = prepare_slice(up_weight.astype(half_type))
    down_slice = prepare_slice(down_weight.astype(half_type).T)
    dy_all = gather_tokens(cot_half.astype(half_type))
    normed_one, inv_one, low_one = rms_forward(hidden, scale_one)
    query = dot(low_one, query_full, ((1,), (0,))).reshape(block, heads_here, HD)
    keyval = dot(low_one, keyval_full, ((1,), (0,)))
    cosine, sine = rope_tables(positions[0])
    query_low = (rotate(query, cosine[:, None, :], sine[:, None, :]) * HD ** (-0.5)).astype(
        half_type
    )
    key_low = rotate(keyval[:, :HD], cosine, sine).astype(half_type)
    keyval_low = jnp.concatenate([key_low, keyval[:, HD:].astype(half_type)], axis=-1)
    keyval_all = lax.all_gather(keyval_low, "context", axis=0, tiled=True)
    keys_all = keyval_all[:, :HD]
    values_all = keyval_all[:, HD:]
    rows_index = context_index * block + jnp.arange(block, dtype=jnp.int32)
    cols_index = jnp.arange(keys_all.shape[0], dtype=jnp.int32)
    allowed = (rows_index[:, None] >= cols_index[None, :]) & (
        segment_ids[0][:, None] == seg_all[0][None, :]
    )
    scores = jnp.einsum("bhd,jd->hbj", query_low, keys_all, preferred_element_type=single)
    masked = jnp.where(allowed, scores, masked_value)
    top = jnp.max(masked, axis=-1, keepdims=True)
    total = jnp.sum(jnp.where(allowed, jnp.exp(masked - top), 0.0), axis=-1, keepdims=True)
    lse = top + jnp.log(total)
    prob = jnp.where(allowed, jnp.exp(masked - lse), 0.0)
    prob_low = prob.astype(half_type)
    att_low = jnp.einsum("hbj,jd->bhd", prob_low, values_all, preferred_element_type=single).astype(
        half_type
    )
    att_flat = att_low.reshape(block, heads_width)
    attn_part = dot(att_flat, output_full, ((1,), (1,)))
    attn_half = lax.psum_scatter(
        attn_part.astype(half_type), "tensor", scatter_dimension=0, tiled=True
    )
    mid_half = hidden_half + attn_half.astype(single)
    normed_two, inv_two, low_two = rms_forward(mid_half, scale_two)
    low_all = gather_tokens(low_two)
    gate = dot(low_all, gate_slice, ((1,), (0,)))
    upper = dot(low_all, up_slice, ((1,), (0,)))
    dhid = dot(dy_all, down_slice, ((1,), (0,)))
    gelu_gate, gelu_back = jax.vjp(gelu_tanh, gate)
    hid_low = (gelu_gate * upper).astype(half_type)
    dgate_low = gelu_back(dhid * upper)[0].astype(half_type)
    dup_low = (dhid * gelu_gate).astype(half_type)
    dnorm_two = scatter_tokens(
        dot(dgate_low, gate_slice, ((1,), (1,))) + dot(dup_low, up_slice, ((1,), (1,)))
    )
    mlp_half = scatter_tokens(dot(hid_low, down_slice, ((1,), (1,))))
    grad_wd = return_slice(dot(dy_all, hid_low, ((0,), (0,)))).T
    grad_wg = return_slice(dot(low_all, dgate_low, ((0,), (0,))))
    grad_wu = return_slice(dot(low_all, dup_low, ((0,), (0,))))
    dmid_norm, terms_two = rms_backward(dnorm_two, normed_two, inv_two, scale_two)
    dmid_half = cot_half + dmid_norm
    dmid_low = lax.all_gather(dmid_half.astype(half_type), "tensor", axis=0, tiled=True)
    grad_out_full = dot(dmid_low, att_flat, ((0,), (0,)))
    datt_low = (
        dot(dmid_low, output_full, ((1,), (0,))).astype(half_type).reshape(block, heads_here, HD)
    )
    delta = jnp.einsum("bhd,bhd->hb", datt_low, att_low, preferred_element_type=single)
    dprob = jnp.einsum("bhd,jd->hbj", datt_low, values_all, preferred_element_type=single)
    dscore_low = (prob * (dprob - delta[..., None])).astype(half_type)
    dquery = jnp.einsum("hbj,jd->bhd", dscore_low, keys_all, preferred_element_type=single)
    dkey_part = jnp.einsum("hbj,bhd->jd", dscore_low, query_low, preferred_element_type=single)
    dvalue_part = jnp.einsum("hbj,bhd->jd", prob_low, datt_low, preferred_element_type=single)
    dkeyval_own = lax.psum_scatter(
        jnp.concatenate([dkey_part, dvalue_part], axis=-1).astype(half_type),
        "context",
        scatter_dimension=0,
        tiled=True,
    )
    dkeyval_sum = lax.psum(dkeyval_own.astype(single), "tensor")
    dquery_low = (
        (unrotate(dquery, cosine[:, None, :], sine[:, None, :]) * HD ** (-0.5))
        .astype(half_type)
        .reshape(block, heads_width)
    )
    dnorm_query = dot(dquery_low, query_full, ((1,), (1,)))
    dnorm_query = lax.psum_scatter(
        dnorm_query.astype(half_type), "tensor", scatter_dimension=0, tiled=True
    ).astype(single)
    dkeyval_low = jnp.concatenate(
        [unrotate(dkeyval_sum[:, :HD], cosine, sine), dkeyval_sum[:, HD:]], axis=-1
    ).astype(half_type)
    dkeyval_half = lax.dynamic_slice_in_dim(dkeyval_low, x * half_rows, half_rows, 0)
    dnorm_one = dnorm_query + dot(dkeyval_half, keyval_full, ((1,), (1,)))
    normed_half = lax.dynamic_slice_in_dim(normed_one, x * half_rows, half_rows, 0)
    inv_half = lax.dynamic_slice_in_dim(inv_one, x * half_rows, half_rows, 0)
    dinput_norm, terms_one = rms_backward(dnorm_one, normed_half, inv_half, scale_one)
    grad_query_full = dot(low_one, dquery_low, ((0,), (0,)))
    grad_keyval_full = dot(low_one, dkeyval_low, ((0,), (0,)))
    grad_wq = scatter_rows(grad_query_full)
    grad_wkv = scatter_rows(grad_keyval_full)
    grad_wo = scatter_rows(grad_out_full).T
    terms = jnp.stack([jnp.sum(terms_one, axis=0), jnp.sum(terms_two, axis=0)])
    terms = lax.psum_scatter(terms, ("fsdp", "context"), scatter_dimension=1, tiled=True)
    terms = lax.psum(terms, "tensor")
    grad_s1, grad_s2 = (terms[0], terms[1])
    outs = jnp.stack([mid_half + mlp_half, dmid_half + dinput_norm])
    outs = lax.all_gather(outs, "tensor", axis=1, tiled=True)
    masters = (
        attn_scale,
        query_weight,
        keyval_weight,
        output_weight,
        mlp_scale,
        gate_weight,
        up_weight,
        down_weight,
    )
    grads = (grad_s1, grad_wq, grad_wkv, grad_wo, grad_s2, grad_wg, grad_wu, grad_wd)
    firsts = (
        first_attn_scale,
        first_query_weight,
        first_keyval_weight,
        first_output_weight,
        first_mlp_scale,
        first_gate_weight,
        first_up_weight,
        first_down_weight,
    )
    seconds = (
        second_attn_scale,
        second_query_weight,
        second_keyval_weight,
        second_output_weight,
        second_mlp_scale,
        second_gate_weight,
        second_up_weight,
        second_down_weight,
    )
    results = [
        adamw(weight, grad, first, second)
        for weight, grad, first, second in zip(masters, grads, firsts, seconds)
    ]
    return (
        outs[0][None],
        outs[1][None],
        *grads,
        *(entry[0] for entry in results),
        *(entry[1] for entry in results),
        *(entry[2] for entry in results),
    )


def solution(mesh):
    both = ("fsdp", "context")
    tokens = P("fsdp", "context", None)
    weights = (
        P(both),
        P(both, "tensor"),
        P(both, None),
        P("tensor", both),
        P(both),
        P(both, "tensor"),
        P(both, "tensor"),
        P("tensor", both),
    )
    return jax.shard_map(
        on_device,
        mesh=mesh,
        in_specs=(tokens, tokens, P("fsdp", "context"), P("fsdp", "context"), *weights * 3),
        out_specs=(tokens, tokens, *weights * 4),
        check_vma=False,
    )
```

profile of v0, /device:TPU:0, one launch (start us, length us, event | category | flops | bytes accessed | tf_op | source)
XLA Modules:
  0.0 1195.5 jit_solution(1834390715932010794)
XLA Ops:
  13.0 34.2 %all-gather = bf16[16,160,2]{1,2,0:T(2,128)(2,1)S(1)} all-gather(bf16[1,160,2]{1,2,0:T(2,128)(2,1)S(1)} %maximum_bitcast_fusion), channel_id=1, replica_groups=mesh['fsdp'=4,'context'=4,'tensor'=2] {'fsdp','context'}, dimensions={0}, use_global_device_ids=true | all-gather | bytes 10880 | tf_op jit(solution)/shard_map/all_gather | solution.py:76
  47.3 7.6 all_gather.42
  60.3 18.9 %all_gather.41 = bf16[512,512]{1,0:T(8,128)(2,1)S(1)} all-gather(bf16[128,512]{1,0:T(8,128)(2,1)S(1)} %pad_maximum_fusion.2), channel_id=1, replica_groups=mesh['fsdp'=4,'context'=4,'tensor'=2] {'context'}, dimensions={0}, use_global_device_ids=true | all-gather | bytes 655360 | tf_op jit(solution)/shard_map/all_gather | solution.py:179
  79.2 45.6 %all-gather.13.cloned.1.call-done = bf16[2560,1280]{1,0:T(8,128)(2,1)} async-done(((bf16[160,1280]{1,0:T(8,128)(2,1)}), bf16[2560,1280]{1,0:T(8,128)(2,1)}) %all-gather.13.cloned.1.call-update) | async-done | bytes 6553616 | tf_op jit(solution)/shard_map/all_gather | solution.py:82
  124.8 9.4 copy.192
  134.3 5.2 fusion.29
  143.0 46.3 %all-gather.15.cloned.1.call-done = bf16[2560,1280]{1,0:T(8,128)(2,1)} async-done(((bf16[160,1280]{1,0:T(8,128)(2,1)}), bf16[2560,1280]{1,0:T(8,128)(2,1)}) %all-gather.15.cloned.1.call-update) | async-done | bytes 6553616 | tf_op jit(solution)/shard_map/all_gather | solution.py:82
  189.3 6.0 convolution_convert_fusion.8
  197.3 2.8 convert_bitcast_fusion.3
  200.1 4.4 reshape.272
  206.3 60.5 %all_to_all.30 = bf16[4,160,960]{2,1,0:T(8,128)(2,1)} all-to-all(bf16[4,160,960]{2,1,0:T(8,128)(2,1)S(1)} %copy.197), channel_id=1, replica_groups=mesh['fsdp'=4,'context'=4,'tensor'=2] {'context'}, dimensions={0} | all-to-all | bytes 2457600 | tf_op jit(solution)/shard_map/all_to_all | solution.py:89
  266.9 2.8 convert_element_type.196
  269.8 4.4 reshape.268
  275.9 33.0 %all_to_all.31 = bf16[4,160,960]{2,1,0:T(8,128)(2,1)} all-to-all(bf16[4,160,960]{2,1,0:T(8,128)(2,1)S(1)} %copy.195), channel_id=1, replica_groups=mesh['fsdp'=4,'context'=4,'tensor'=2] {'context'}, dimensions={0} | all-to-all | bytes 2457600 | tf_op jit(solution)/shard_map/all_to_all | solution.py:89
  311.2 2.8 convert_element_type.197
  314.0 4.4 reshape.270
  320.3 33.4 %all_to_all.32 = bf16[4,160,960]{2,1,0:T(8,128)(2,1)} all-to-all(bf16[4,160,960]{2,1,0:T(8,128)(2,1)S(1)} %copy.196), channel_id=1, replica_groups=mesh['fsdp'=4,'context'=4,'tensor'=2] {'context'}, dimensions={0} | all-to-all | bytes 2457600 | tf_op jit(solution)/shard_map/all_to_all | solution.py:89
  354.3 7.3 fusion.80
  361.6 47.2 %all-gather.17.cloned.1.call-done = bf16[512,2560]{1,0:T(8,128)(2,1)} async-done(((bf16[64,2560]{1,0:T(8,128)(2,1)}), bf16[512,2560]{1,0:T(8,128)(2,1)}) %all-gather.17.cloned.1.call-update) | async-done | bytes 2621456 | tf_op jit(solution)/shard_map/all_gather | solution.py:95
  408.8 7.3 fusion.79
  416.1 33.2 %all-gather.21.cloned.1.call-done = bf16[16,160,960]{2,1,0:T(8,128)(2,1)} async-done(((bf16[4,160,960]{2,1,0:T(8,128)(2,1)}), bf16[16,160,960]{2,1,0:T(8,128)(2,1)}) %all-gather.21.cloned.1.call-update) | async-done | bytes 4915216 | tf_op jit(solution)/shard_map/all_gather | solution.py:90
  449.3 9.6 multiply_convert_fusion.1
  458.9 3.1 fusion.81
  462.1 4.4 add_convert_fusion
  466.6 7.2 convolution_convert_fusion.5
  473.9 63.9 %reduce-scatter.19.cloned.1.call-done = bf16[64,2560]{1,0:T(8,128)(2,1)} async-done(((bf16[512,2560]{1,0:T(8,128)(2,1)}), bf16[64,2560]{1,0:T(8,128)(2,1)}) %reduce-scatter.19.cloned.1.call-update) | async-done | bytes 327696 | tf_op jit(solution)/shard_map/reduce_scatter | solution.py:99
  539.1 72.4 %reduce-scatter.17.cloned.1.call-done = bf16[64,2560]{1,0:T(8,128)(2,1)} async-done(((bf16[512,2560]{1,0:T(8,128)(2,1)}), bf16[64,2560]{1,0:T(8,128)(2,1)}) %reduce-scatter.17.cloned.1.call-update) | async-done | bytes 327696 | tf_op jit(solution)/shard_map/reduce_scatter | solution.py:99
  613.8 8.7 all_gather.50
  623.4 4.6 convolution_convert_fusion.9
  639.5 6.2 convolution_convert_fusion.7
  645.8 7.0 convolution_convert_fusion.4
  652.8 7.7 copy.209
  660.8 7.0 convolution_convert_fusion.3
  667.8 7.9 copy.211
  676.4 13.2 %all-reduce.1 = f32[128,512]{1,0:T(8,128)S(1)} all-reduce(bf16[128,512]{1,0:T(8,128)(2,1)} %reduce-scatter.23.cloned.1.call-done), channel_id=1, replica_groups=mesh['fsdp'=4,'context'=4,'tensor'=2] {'tensor'}, use_global_device_ids=true, to_apply=%region_10.11 | all-reduce | flops 65536 | bytes 393216 | tf_op jit(solution)/shard_map/psum | solution.py:238
  691.3 3.6 multiply_reduce_fusion
  696.6 7.0 convolution_convert_fusion.2
  703.6 7.8 copy.213
  717.9 4.6 convolution_convert_fusion.1
  722.6 4.9 reduce-scatter.31.cloned.1.call-done
  727.5 4.6 all-to-all-start.3
  732.1 4.9 convolution_convert_fusion
  737.2 44.2 %reduce-scatter.33.cloned.1.call-done = bf16[4,160,960]{2,1,0:T(8,128)(2,1)} async-done(((bf16[16,160,960]{2,1,0:T(8,128)(2,1)}), bf16[4,160,960]{2,1,0:T(8,128)(2,1)}) %reduce-scatter.33.cloned.1.call-update) | async-done | bytes 1228816 | tf_op jit(solution)/shard_map/reduce_scatter | solution.py:116
  781.4 4.6 all-to-all-start.4
  786.0 58.0 %reduce-scatter.37.cloned.1.call-done = f32[160,2]{1,0:T(8,128)} async-done(((f32[2560,2]{1,0:T(8,128)}), f32[160,2]{1,0:T(8,128)}) %reduce-scatter.37.cloned.1.call-update) | async-done | bytes 1296
  845.0 4.9 psum.15
  849.9 47.0 %reduce-scatter.35.cloned.1.call-done = bf16[4,160,960]{2,1,0:T(8,128)(2,1)} async-done(((bf16[16,160,960]{2,1,0:T(8,128)(2,1)}), bf16[4,160,960]{2,1,0:T(8,128)(2,1)}) %reduce-scatter.35.cloned.1.call-update) | async-done | bytes 1228816 | tf_op jit(solution)/shard_map/reduce_scatter | solution.py:116
  896.9 5.0 all-to-all-start.5
  902.6 35.4 %all-gather.27.cloned.1.call-done = f32[2,128,2560]{2,1,0:T(8,128)} async-done(((f32[2,64,2560]{2,1,0:T(8,128)}), f32[2,128,2560]{2,1,0:T(8,128)}) %all-gather.27.cloned.1.call-update) | async-done | bytes 2621456 | tf_op jit(solution)/shard_map/all_gather | solution.py:266
  938.1 3.4 fusion.76
  941.4 64.5 %reduce-scatter.27.cloned.1.call-done = bf16[160,512]{1,0:T(8,128)(2,1)} async-done(((bf16[2560,512]{1,0:T(8,128)(2,1)}), bf16[160,512]{1,0:T(8,128)(2,1)}) %reduce-scatter.27.cloned.1.call-update) | async-done | bytes 163856 | tf_op jit(solution)/shard_map/reduce_scatter | solution.py:105
  1008.4 3.2 copy.210
  1011.6 4.2 reshape.278
  1017.6 3.2 copy.212
  1020.7 4.4 reshape.279
  1026.9 3.2 copy.214
  1030.0 4.6 reshape.280
  1034.7 7.8 multiply_subtract_fusion.2
  1043.6 4.5 multiply_subtract_fusion.1
  1050.1 4.2 multiply_subtract_fusion
  1054.4 41.3 %reduce-scatter.25.cloned.1.call-done = bf16[160,1280]{1,0:T(8,128)(2,1)} async-done(((bf16[2560,1280]{1,0:T(8,128)(2,1)}), bf16[160,1280]{1,0:T(8,128)(2,1)}) %reduce-scatter.25.cloned.1.call-update) | async-done | bytes 409616 | tf_op jit(solution)/shard_map/reduce_scatter | solution.py:105
  1095.7 3.4 multiply_subtract_fusion.4
  1099.1 86.2 %reduce-scatter.29.cloned.1.call-done = bf16[160,1280]{1,0:T(8,128)(2,1)} async-done(((bf16[2560,1280]{1,0:T(8,128)(2,1)}), bf16[160,1280]{1,0:T(8,128)(2,1)}) %reduce-scatter.29.cloned.1.call-update) | async-done | bytes 409616 | tf_op jit(solution)/shard_map/reduce_scatter | solution.py:105
  1185.3 2.9 multiply_subtract_fusion.3
  (266 shorter events, 61.2 us)
Async XLA Ops:
  8.1 4.9 copy-start.61
  8.1 4.9 copy-start.63
  8.1 39.2 %copy-start.60 = (s32[1,128]{1,0:T(1,128)S(1)}, s32[1,128]{1,0:T(1,128)}, u32[]{:S(2)}) copy-start(s32[1,128]{1,0:T(1,128)} %param.30) | copy-start | bytes 1540
  8.1 47.4 %copy-start = (f32[1,128,2560]{2,1,0:T(8,128)S(1)}, f32[1,128,2560]{2,1,0:T(8,128)}, u32[]{:S(2)}) copy-start(f32[1,128,2560]{2,1,0:T(8,128)} %param.28) | copy-start | bytes 3932164
  8.1 49.6 %all-gather.11.cloned.1.call-start = ((), (), s32[]{:S(2)}) async-start(), calls=%async_computation.18 | async-start | bytes 2785280 | tf_op jit(solution)/shard_map/all_gather | solution.py:82
  9.9 45.7 %copy-start.71 = (s32[1,128]{1,0:T(1,128)S(1)}, s32[1,128]{1,0:T(1,128)}, u32[]{:S(2)}) copy-start(s32[1,128]{1,0:T(1,128)} %param.31) | copy-start | bytes 1540
  10.0 114.8 %all-gather.13.cloned.1.call-start = ((), (), s32[]{:S(2)}) async-start(), calls=%async_computation.19 | async-start | bytes 6963200 | tf_op jit(solution)/shard_map/all_gather | solution.py:82
  12.0 177.3 %all-gather.15.cloned.1.call-start = ((), (), s32[]{:S(2)}) async-start(), calls=%async_computation.20 | async-start | bytes 6963200 | tf_op jit(solution)/shard_map/all_gather | solution.py:82
  12.9 296.2 %reduce-scatter.15.cloned.1.call-start = ((), (), s32[]{:S(2)}) async-start(), calls=%async_computation.21 | async-start | bytes 983040 | tf_op jit(solution)/shard_map/reduce_scatter | solution.py:199
  54.9 5.1 copy-start.56
  55.7 78.6 %copy-start.50 = (f32[128]{0:T(128)}, f32[128]{0:T(128)S(1)}, u32[]{:S(2)}) copy-start(f32[128]{0:T(128)S(1)} %add_rsqrt_fusion.1) | copy-start | bytes 1540
  55.9 84.2 %copy-start.39 = (pred[128,512]{0,1:T(8,128)(4,1)}, pred[128,512]{0,1:T(8,128)(4,1)S(1)}, u32[]{:S(2)}) copy-start(pred[128,512]{0,1:T(8,128)(4,1)S(1)} %fusion.33) | copy-start | bytes 196612
  60.3 79.2 %copy-start.37 = (f32[128,128]{1,0:T(8,128)}, f32[128,128]{1,0:T(8,128)S(1)}, u32[]{:S(2)}) copy-start(f32[128,128]{1,0:T(8,128)S(1)} %get-tuple-element.87) | copy-start | bytes 196612
  79.2 61.1 %copy-start.24 = (bf16[512,512]{1,0:T(8,128)(2,1)}, bf16[512,512]{1,0:T(8,128)(2,1)S(1)}, u32[]{:S(2)}) copy-start(bf16[512,512]{1,0:T(8,128)(2,1)S(1)} %all_gather.41) | copy-start | bytes 1572868
  143.0 52.3 %copy-start.15 = (bf16[256,5,128]{2,0,1:T(8,128)(2,1)}, bf16[256,5,128]{2,0,1:T(8,128)(2,1)S(1)}, u32[]{:S(2)}) copy-start(bf16[256,5,128]{2,0,1:T(8,128)(2,1)S(1)} %convolution_convert_fusion.10) | copy-start | bytes 983044
  195.3 159.0 %all-gather.25.cloned.1.call-start = ((), (), s32[]{:S(2)}) async-start(), calls=%async_computation.27 | async-start | bytes 2949120 | tf_op jit(solution)/shard_map/all_gather | solution.py:95
  197.2 157.1 %all-gather.23.cloned.1.call-start = ((), (), s32[]{:S(2)}) async-start(), calls=%async_computation.25 | async-start | bytes 6553600 | tf_op jit(solution)/shard_map/all_gather | solution.py:90
  266.9 94.7 %all-gather.19.cloned.1.call-start = ((), (), s32[]{:S(2)}) async-start(), calls=%async_computation.23 | async-start | bytes 6553600 | tf_op jit(solution)/shard_map/all_gather | solution.py:90
  275.9 34.3 %copy-start.43 = (f32[2560]{0:T(1024)S(1)}, f32[2560]{0:T(1024)}, u32[]{:S(2)}) copy-start(f32[2560]{0:T(1024)} %get-tuple-element.38) | copy-start | bytes 30724
  309.0 99.9 %all-gather.17.cloned.1.call-start = ((), (), s32[]{:S(2)}) async-start(), calls=%async_computation.22 | async-start | bytes 2949120 | tf_op jit(solution)/shard_map/all_gather | solution.py:95
  311.1 138.2 %all-gather.21.cloned.1.call-start = ((), (), s32[]{:S(2)}) async-start(), calls=%async_computation.24 | async-start | bytes 6553600 | tf_op jit(solution)/shard_map/all_gather | solution.py:90
  353.7 184.0 %reduce-scatter.19.cloned.1.call-start = ((), (), s32[]{:S(2)}) async-start(), calls=%async_computation.28 | async-start | bytes 2949120 | tf_op jit(solution)/shard_map/reduce_scatter | solution.py:99
  449.3 9.6 copy-start.69
  466.5 144.9 %reduce-scatter.17.cloned.1.call-start = ((), (), s32[]{:S(2)}) async-start(), calls=%async_computation.26 | async-start | bytes 2949120 | tf_op jit(solution)/shard_map/reduce_scatter | solution.py:99
  473.8 202.6 %reduce-scatter.23.cloned.1.call-start = ((), (), s32[]{:S(2)}) async-start(), calls=%async_computation.30 | async-start | bytes 655360 | tf_op jit(solution)/shard_map/reduce_scatter | solution.py:232
  539.1 74.8 %copy-start.58 = (f32[64]{0:T(128)}, f32[64]{0:T(128)S(1)}, u32[]{:S(2)}) copy-start(f32[64]{0:T(128)S(1)} %broadcast_multiply_fusion.1) | copy-start | bytes 772
  623.4 6.5 copy-start.40
  623.4 6.5 copy-start.55
  635.2 56.1 %reduce-scatter.21.cloned.1.call-start = ((), (), s32[]{:S(2)}) async-start(), calls=%async_computation.29 | async-start | bytes 983040 | tf_op jit(solution)/shard_map/reduce_scatter | solution.py:245
  645.7 81.8 %reduce-scatter.31.cloned.1.call-start = ((), (), s32[]{:S(2)}) async-start(), calls=%async_computation.35 | async-start | bytes 6553600 | tf_op jit(solution)/shard_map/reduce_scatter | solution.py:116
  660.6 120.8 %reduce-scatter.33.cloned.1.call-start = ((), (), s32[]{:S(2)}) async-start(), calls=%async_computation.36 | async-start | bytes 6553600 | tf_op jit(solution)/shard_map/reduce_scatter | solution.py:116
  675.7 168.3 %reduce-scatter.37.cloned.1.call-start = ((), (), s32[]{:S(2)}) async-start(), calls=%async_computation.38 | async-start | bytes 1392640
  696.6 200.4 %reduce-scatter.35.cloned.1.call-start = ((), (), s32[]{:S(2)}) async-start(), calls=%async_computation.37 | async-start | bytes 6553600 | tf_op jit(solution)/shard_map/reduce_scatter | solution.py:116
  711.5 226.5 %all-gather.27.cloned.1.call-start = ((), (), s32[]{:S(2)}) async-start(), calls=%async_computation.31 | async-start | bytes 3932160 | tf_op jit(solution)/shard_map/all_gather | solution.py:266
  715.3 290.7 %reduce-scatter.27.cloned.1.call-start = ((), (), s32[]{:S(2)}) async-start(), calls=%async_computation.33 | async-start | bytes 2785280 | tf_op jit(solution)/shard_map/reduce_scatter | solution.py:105
  717.8 377.9 %reduce-scatter.25.cloned.1.call-start = ((), (), s32[]{:S(2)}) async-start(), calls=%async_computation.32 | async-start | bytes 6963200 | tf_op jit(solution)/shard_map/reduce_scatter | solution.py:105
  722.5 9.6 copy-start.7
  722.6 9.6 copy-start.17
  727.5 53.9 %all-to-all-start.3 = ((bf16[4,160,960]{2,1,0:T(8,128)(2,1)}), bf16[4,160,960]{2,1,0:T(8,128)(2,1)S(1)}, u32[]{:S(2)}, u32[]{:S(2)}) async-start(bf16[4,160,960]{2,1,0:T(8,128)(2,1)} %reduce-scatter.31.cloned.1.call-done), calls=%async_computation.12 | async-start | bytes 2621440 | tf_op jit(solution)/shard_map/all_to_all | solution.py:117
  732.1 453.2 %reduce-scatter.29.cloned.1.call-start = ((), (), s32[]{:S(2)}) async-start(), calls=%async_computation.34 | async-start | bytes 6963200 | tf_op jit(solution)/shard_map/reduce_scatter | solution.py:105
  737.1 164.9 %copy-start.62 = (f32[160]{0:T(256)S(1)}, f32[160]{0:T(256)}, u32[]{:S(2)}) copy-start(f32[160]{0:T(256)} %param.36) | copy-start | bytes 1924
  737.1 164.9 %copy-start.64 = (f32[160]{0:T(256)S(1)}, f32[160]{0:T(256)}, u32[]{:S(2)}) copy-start(f32[160]{0:T(256)} %param.32) | copy-start | bytes 1924
  737.1 164.9 %copy-start.65 = (f32[160]{0:T(256)S(1)}, f32[160]{0:T(256)}, u32[]{:S(2)}) copy-start(f32[160]{0:T(256)} %param.44) | copy-start | bytes 1924
  737.1 164.8 %copy-start.66 = (f32[160]{0:T(256)S(1)}, f32[160]{0:T(256)}, u32[]{:S(2)}) copy-start(f32[160]{0:T(256)} %param.52) | copy-start | bytes 1924
  737.1 164.8 %copy-start.67 = (f32[160]{0:T(256)S(1)}, f32[160]{0:T(256)}, u32[]{:S(2)}) copy-start(f32[160]{0:T(256)} %param.48) | copy-start | bytes 1924
  737.2 164.8 %copy-start.68 = (f32[160]{0:T(256)S(1)}, f32[160]{0:T(256)}, u32[]{:S(2)}) copy-start(f32[160]{0:T(256)} %param.40) | copy-start | bytes 1924
  781.4 115.5 %copy-start.10 = (bf16[4,160,960]{2,1,0:T(8,128)(2,1)}, bf16[4,160,960]{2,1,0:T(8,128)(2,1)S(1)}, u32[]{:S(2)}) copy-start(bf16[4,160,960]{2,1,0:T(8,128)(2,1)S(1)} %all-to-all-done.3) | copy-start | bytes 3686404
  781.4 115.5 %all-to-all-start.4 = ((bf16[4,160,960]{2,1,0:T(8,128)(2,1)}), bf16[4,160,960]{2,1,0:T(8,128)(2,1)}, u32[]{:S(2)}, u32[]{:S(2)}) async-start(bf16[4,160,960]{2,1,0:T(8,128)(2,1)} %reduce-scatter.33.cloned.1.call-done), calls=%async_computation.14 | async-start | bytes 2621440 | tf_op jit(solution)/shard_map/all_to_all | solution.py:117
  849.9 91.5 %copy-start.52 = (f32[1,160]{1,0:T(1,128)}, f32[1,160]{1,0:T(1,128)S(1)}, u32[]{:S(2)}) copy-start(f32[1,160]{1,0:T(1,128)S(1)} %get-tuple-element.84) | copy-start | bytes 1924
  849.9 91.5 %copy-start.53 = (f32[1,160]{1,0:T(1,128)}, f32[1,160]{1,0:T(1,128)S(1)}, u32[]{:S(2)}) copy-start(f32[1,160]{1,0:T(1,128)S(1)} %get-tuple-element.85) | copy-start | bytes 1924
  896.9 128.2 %all-to-all-start.5 = ((bf16[4,160,960]{2,1,0:T(8,128)(2,1)}), bf16[4,160,960]{2,1,0:T(8,128)(2,1)}, u32[]{:S(2)}, u32[]{:S(2)}) async-start(bf16[4,160,960]{2,1,0:T(8,128)(2,1)} %reduce-scatter.35.cloned.1.call-done), calls=%async_computation.16 | async-start | bytes 2621440 | tf_op jit(solution)/shard_map/all_to_all | solution.py:117
  902.6 103.3 %copy-start.26 = (f32[160,512]{1,0:T(8,128)S(1)}, f32[160,512]{1,0:T(8,128)}, u32[]{:S(2)}) copy-start(f32[160,512]{1,0:T(8,128)} %param.34) | copy-start | bytes 983044
  902.6 103.3 %copy-start.41 = (f32[160,512]{1,0:T(8,128)S(1)}, f32[160,512]{1,0:T(8,128)}, u32[]{:S(2)}) copy-start(f32[160,512]{1,0:T(8,128)} %param.42) | copy-start | bytes 983044
  902.6 103.3 %copy-start.42 = (f32[160,512]{1,0:T(8,128)S(1)}, f32[160,512]{1,0:T(8,128)}, u32[]{:S(2)}) copy-start(f32[160,512]{1,0:T(8,128)} %param.50) | copy-start | bytes 983044
  1034.6 7.8 copy-start.2
  1034.6 7.8 copy-start.4
  1034.6 7.8 copy-start.20
  1034.6 8.9 copy-start.21
  1043.6 5.8 copy-start.22
  1043.6 6.5 copy-start.23
  1050.1 45.6 %copy-start.12 = (f32[160,1280]{1,0:T(8,128)S(1)}, f32[160,1280]{1,0:T(8,128)}, u32[]{:S(2)}) copy-start(f32[160,1280]{1,0:T(8,128)} %param.33) | copy-start | bytes 2457604
  1054.4 130.9 %copy-start.14 = (f32[1280,160]{0,1:T(8,128)S(1)}, f32[1280,160]{0,1:T(8,128)}, u32[]{:S(2)}) copy-start(f32[1280,160]{0,1:T(8,128)} %param.35) | copy-start | bytes 2457604
  1054.4 130.9 %copy-start.32 = (f32[1280,160]{0,1:T(8,128)S(1)}, f32[1280,160]{0,1:T(8,128)}, u32[]{:S(2)}) copy-start(f32[1280,160]{0,1:T(8,128)} %param.43) | copy-start | bytes 2457604
  1054.4 130.9 %copy-start.33 = (f32[1280,160]{0,1:T(8,128)S(1)}, f32[1280,160]{0,1:T(8,128)}, u32[]{:S(2)}) copy-start(f32[1280,160]{0,1:T(8,128)} %param.51) | copy-start | bytes 2457604
  (34 other events, 77.3 us)
Sparse Core Ops, SparseCore 0:
  11.8 45.8 all-gather.10
  60.5 64.2 all-gather.12
  127.7 61.5 all-gather.14
  195.4 15.1 reduce-scatter.14
  635.3 21.1 reduce-scatter.22
  659.2 14.3 reduce-scatter.20
  676.1 51.3 reduce-scatter.30
  730.0 51.3 reduce-scatter.32
  785.6 58.3 reduce-scatter.36
  846.4 50.4 reduce-scatter.34
  899.0 38.9 all-gather.26
  941.7 64.1 reduce-scatter.26
  1009.9 85.7 reduce-scatter.24
  1099.5 85.7 reduce-scatter.28
Sparse Core Ops, SparseCore 1:
  198.5 71.3 all-gather.24
  271.3 38.4 all-gather.22
  311.2 40.2 all-gather.18
  354.3 54.4 all-gather.16
  410.4 38.8 all-gather.20
  466.6 71.1 reduce-scatter.18
  541.1 70.3 reduce-scatter.16
where the time goes:
time: 1210 us; the launch traced here: 1200 us
  waiting for transfers between devices  692 us (57%)
  blocking collectives  214 us (18%)
  matrix products  106 us (9%)
  local copies, waits for them, and re-layouts  93.6 us (8%)
  other arithmetic  56.7 us (5%)
  between operations  16.8 us (1%)
  starting transfers between devices  15.7 us (1%)
    reduce_scatter x3, waiting for transfers between devices, scatter_rows(): lax.psum_scatter(part.astype(half_type), ('fsdp', 'context'), scatter_dim...  192 us
    reduce_scatter x2, waiting for transfers between devices, scatter_tokens(): lax.psum_scatter(part.astype(half_type), ('context', 'tensor'), scatter_d...  136 us
    all_to_all x3, blocking collectives, prepare_slice(): lax.all_to_all(parts, 'context', split_axis=0, concat_axis=0, tiled=True)  127 us
    dot_general x18, matrix products, dot(): lax.dot_general(a, b, (dims, ((), ())), preferred_element_type=single)  100 us
    reduce_scatter x3, waiting for transfers between devices, return_slice(): parts = lax.psum_scatter(parts, 'fsdp', scatter_dimension=0, tiled=True)  96.2 us
    all_gather x3, waiting for transfers between devices, gather_rows(): return lax.all_gather(block, ('fsdp', 'context'), axis=0, tiled=True)  93.5 us
    unnamed x22, waiting for transfers between devices  58.4 us
    all_gather x2, waiting for transfers between devices, gather_tokens(): return lax.all_gather(block, ('context', 'tensor'), axis=0, tiled=True)  47.3 us
  transfers between devices with their start and end apart: 24, of which 15 were waited for; matrix products, arithmetic and copies ran while one was open for 17% of the time, Pallas kernels for 0%

commit v1 on v0

--- a/solution.py
+++ b/solution.py
@@ -17,6 +17,21 @@
 half_type = jnp.bfloat16
 
 
+def panels_rest(matrix, named_axis):
+    tall = jax.lax.axis_size(named_axis)
+    outer, next_value = (tall, jax.lax.axis_index(named_axis))
+    all_rows, found_now = (matrix, 1)
+    while found_now < outer:
+        y2 = jax.lax.ppermute(
+            all_rows, named_axis, tuple(((t, t ^ found_now) for t in range(outer)))
+        )
+        local_part = jnp.concatenate([all_rows, y2], 0)
+        w1 = jnp.concatenate([y2, all_rows], 0)
+        all_rows = jnp.where(next_value & found_now == 0, local_part, w1)
+        found_now = 2 * found_now
+    return all_rows
+
+
 def gelu_tanh(values):
     return jax.nn.gelu(values, approximate=True)
 
@@ -79,7 +94,7 @@
 
 
 def gather_rows(block):
-    return lax.all_gather(block, ("fsdp", "context"), axis=0, tiled=True)
+    return panels_rest(block, ("fsdp", "context"))
 
 
 def prepare_slice(block):

time: 1210 us -> 1340 us (1.11)
  waiting for transfers between devices: 692 us -> 794 us
  other arithmetic: 56.7 us -> 80.9 us
  starting transfers between devices: 15.7 us -> 30.5 us
    ppermute x0 -> x12, waiting for transfers between devices: none -> 193 us  [panels_rest(): jax.lax.ppermute(all_rows, named_axis, tuple(((t, t ^ found_now) for t in...]
    all_gather x3 -> x0, waiting for transfers between devices: 93.5 us -> none  [gather_rows(): return lax.all_gather(block, ('fsdp', 'context'), axis=0, tiled=True)]
    select_n x0 -> x9, other arithmetic: none -> 15.7 us  [panels_rest(): all_rows = jnp.where(next_value & found_now == 0, local_part, w1)]
    ppermute x0 -> x12, starting transfers between devices: none -> 14.8 us  [panels_rest(): jax.lax.ppermute(all_rows, named_axis, tuple(((t, t ^ found_now) for t in...]
    unnamed x22 -> x19, waiting for transfers between devices: 58.4 us -> 58.3 us
  transfers between devices with their start and end apart: 24 -> 33, of which waited for: 15 -> 18; matrix products, arithmetic and copies ran while one was open for 17% -> 17% of each run, Pallas kernels for 0% -> 0%
where the time goes in v1:
time: 1340 us; the launch traced here: 1330 us
  waiting for transfers between devices  794 us (59%)
  blocking collectives  207 us (15%)
  matrix products  111 us (8%)
  local copies, waits for them, and re-layouts  93 us (7%)
  other arithmetic  80.9 us (6%)
  starting transfers between devices  30.5 us (2%)
  between operations  16.7 us (1%)
    reduce_scatter x3, waiting for transfers between devices, scatter_rows(): lax.psum_scatter(part.astype(half_type), ('fsdp', 'context'), scatter_dim...  193 us
    ppermute x12, waiting for transfers between devices, panels_rest(): jax.lax.ppermute(all_rows, named_axis, tuple(((t, t ^ found_now) for t in...  193 us
    reduce_scatter x2, waiting for transfers between devices, scatter_tokens(): lax.psum_scatter(part.astype(half_type), ('context', 'tensor'), scatter_d...  136 us
    all_to_all x3, blocking collectives, prepare_slice(): lax.all_to_all(parts, 'context', split_axis=0, concat_axis=0, tiled=True)  124 us
    dot_general x18, matrix products, dot(): lax.dot_general(a, b, (dims, ((), ())), preferred_element_type=single)  106 us
    reduce_scatter x3, waiting for transfers between devices, return_slice(): parts = lax.psum_scatter(parts, 'fsdp', scatter_dimension=0, tiled=True)  94.4 us
    unnamed x19, waiting for transfers between devices  58.3 us
    all_gather x2, waiting for transfers between devices, gather_tokens(): return lax.all_gather(block, ('context', 'tensor'), axis=0, tiled=True)  50.5 us
  transfers between devices with their start and end apart: 33, of which 18 were waited for; matrix products, arithmetic and copies ran while one was open for 17% of the time, Pallas kernels for 0%

profile of v1, /device:TPU:0, one launch (start us, length us, event | category | flops | bytes accessed | tf_op | source)
XLA Modules:
  0.0 1333.7 jit_solution(13122021714803440177)
XLA Ops:
  12.5 9.5 collective-permute-done.4
  27.3 32.9 %collective-permute-done.5 = bf16[320,1280]{1,0:T(8,128)(2,1)} collective-permute-done((bf16[320,1280]{1,0:T(8,128)(2,1)S(1)}, bf16[320,1280]{1,0:T(8,128)(2,1)}, u32[]{:S(2)}, u32[]{:S(2)}) %collective-permute-start.5) | collective-permute-done | bytes 819232 | tf_op jit(solution)/shard_map/ppermute | solution.py:25
  62.7 32.9 %all-gather = bf16[16,160,2]{1,2,0:T(2,128)(2,1)S(1)} all-gather(bf16[1,160,2]{1,2,0:T(2,128)(2,1)S(1)} %maximum_bitcast_fusion), channel_id=1, replica_groups=mesh['fsdp'=4,'context'=4,'tensor'=2] {'fsdp','context'}, dimensions={0}, use_global_device_ids=true | all-gather | bytes 10880 | tf_op jit(solution)/shard_map/all_gather | solution.py:91
  96.4 7.8 all_gather.32
  113.0 25.6 %collective-permute-done.1 = bf16[320,512]{1,0:T(8,128)(2,1)S(1)} collective-permute-done((bf16[320,512]{1,0:T(8,128)(2,1)S(1)}, bf16[320,512]{1,0:T(8,128)(2,1)S(1)}, u32[]{:S(2)}, u32[]{:S(2)}) %collective-permute-start.1) | collective-permute-done | bytes 327712 | tf_op jit(solution)/shard_map/ppermute | solution.py:25
  138.9 3.5 maximum_select_fusion.2
  146.0 10.0 collective-permute-done.9
  158.6 85.5 %collective-permute-done.3 = bf16[1280,512]{1,0:T(8,128)(2,1)} collective-permute-done((bf16[1280,512]{1,0:T(8,128)(2,1)}, bf16[1280,512]{1,0:T(8,128)(2,1)}, u32[]{:S(2)}, u32[]{:S(2)}) %collective-permute-start.3) | collective-permute-done | bytes 1310752 | tf_op jit(solution)/shard_map/ppermute | solution.py:25
  251.2 15.5 %all_gather.31 = bf16[512,512]{1,0:T(8,128)(2,1)S(1)} all-gather(bf16[128,512]{1,0:T(8,128)(2,1)S(1)} %pad_maximum_fusion.2), channel_id=1, replica_groups=mesh['fsdp'=4,'context'=4,'tensor'=2] {'context'}, dimensions={0}, use_global_device_ids=true | all-gather | bytes 655360 | tf_op jit(solution)/shard_map/all_gather | solution.py:194
  266.7 9.6 fusion.17
  276.4 9.5 copy.233
  285.8 5.1 fusion.30
  293.1 29.5 %collective-permute-done.11 = bf16[1280,1280]{1,0:T(8,128)(2,1)} collective-permute-done((bf16[1280,1280]{1,0:T(8,128)(2,1)}, bf16[1280,1280]{1,0:T(8,128)(2,1)}, u32[]{:S(2)}, u32[]{:S(2)}) %collective-permute-start.11) | collective-permute-done | bytes 3276832 | tf_op jit(solution)/shard_map/ppermute | solution.py:25
  322.5 7.2 convolution_convert_fusion.8
  335.1 4.4 reshape.272
  341.2 60.0 %all_to_all.30 = bf16[4,160,960]{2,1,0:T(8,128)(2,1)} all-to-all(bf16[4,160,960]{2,1,0:T(8,128)(2,1)S(1)} %copy.238), channel_id=1, replica_groups=mesh['fsdp'=4,'context'=4,'tensor'=2] {'context'}, dimensions={0} | all-to-all | bytes 2457600 | tf_op jit(solution)/shard_map/all_to_all | solution.py:104
  404.1 4.4 reshape.268
  410.2 31.4 %all_to_all.31 = bf16[4,160,960]{2,1,0:T(8,128)(2,1)} all-to-all(bf16[4,160,960]{2,1,0:T(8,128)(2,1)S(1)} %copy.236), channel_id=1, replica_groups=mesh['fsdp'=4,'context'=4,'tensor'=2] {'context'}, dimensions={0} | all-to-all | bytes 2457600 | tf_op jit(solution)/shard_map/all_to_all | solution.py:104
  446.6 4.4 reshape.270
  452.8 32.8 %all_to_all.32 = bf16[4,160,960]{2,1,0:T(8,128)(2,1)} all-to-all(bf16[4,160,960]{2,1,0:T(8,128)(2,1)S(1)} %copy.237), channel_id=1, replica_groups=mesh['fsdp'=4,'context'=4,'tensor'=2] {'context'}, dimensions={0} | all-to-all | bytes 2457600 | tf_op jit(solution)/shard_map/all_to_all | solution.py:104
  486.0 7.3 fusion.87
  493.3 50.5 %all-gather.8.cloned.1.call-done = bf16[512,2560]{1,0:T(8,128)(2,1)} async-done(((bf16[64,2560]{1,0:T(8,128)(2,1)}), bf16[512,2560]{1,0:T(8,128)(2,1)}) %all-gather.8.cloned.1.call-update) | async-done | bytes 2621456 | tf_op jit(solution)/shard_map/all_gather | solution.py:110
  543.8 7.3 fusion.86
  551.1 33.2 %all-gather.12.cloned.1.call-done = bf16[16,160,960]{2,1,0:T(8,128)(2,1)} async-done(((bf16[4,160,960]{2,1,0:T(8,128)(2,1)}), bf16[16,160,960]{2,1,0:T(8,128)(2,1)}) %all-gather.12.cloned.1.call-update) | async-done | bytes 4915216 | tf_op jit(solution)/shard_map/all_gather | solution.py:105
  584.3 9.6 multiply_convert_fusion.1
  593.9 3.2 fusion.88
  597.1 4.3 add_convert_fusion
  601.5 7.2 convolution_convert_fusion.5
  608.8 63.9 %reduce-scatter.19.cloned.1.call-done = bf16[64,2560]{1,0:T(8,128)(2,1)} async-done(((bf16[512,2560]{1,0:T(8,128)(2,1)}), bf16[64,2560]{1,0:T(8,128)(2,1)}) %reduce-scatter.19.cloned.1.call-update) | async-done | bytes 327696 | tf_op jit(solution)/shard_map/reduce_scatter | solution.py:114
  674.0 72.0 %reduce-scatter.17.cloned.1.call-done = bf16[64,2560]{1,0:T(8,128)(2,1)} async-done(((bf16[512,2560]{1,0:T(8,128)(2,1)}), bf16[64,2560]{1,0:T(8,128)(2,1)}) %reduce-scatter.17.cloned.1.call-update) | async-done | bytes 327696 | tf_op jit(solution)/shard_map/reduce_scatter | solution.py:114
  748.3 8.7 all_gather.38
  757.8 6.8 convolution_convert_fusion.9
  776.4 7.2 convolution_convert_fusion.7
  783.7 7.0 convolution_convert_fusion.4
  790.7 7.8 copy.250
  798.9 7.0 convolution_convert_fusion.3
  806.0 7.9 copy.252
  814.5 13.4 %all-reduce.1 = f32[128,512]{1,0:T(8,128)S(1)} all-reduce(bf16[128,512]{1,0:T(8,128)(2,1)} %reduce-scatter.23.cloned.1.call-done), channel_id=1, replica_groups=mesh['fsdp'=4,'context'=4,'tensor'=2] {'tensor'}, use_global_device_ids=true, to_apply=%region_10.11 | all-reduce | flops 65536 | bytes 393216 | tf_op jit(solution)/shard_map/psum | solution.py:253
  829.6 4.7 multiply_reduce_fusion
  836.0 7.0 convolution_convert_fusion.2
  843.0 7.8 copy.254
  857.2 4.7 convolution_convert_fusion.1
  861.9 3.2 reduce-scatter.31.cloned.1.call-done
  865.2 4.6 all-to-all-start.3
  869.8 4.9 convolution_convert_fusion
  874.8 44.1 %reduce-scatter.33.cloned.1.call-done = bf16[4,160,960]{2,1,0:T(8,128)(2,1)} async-done(((bf16[16,160,960]{2,1,0:T(8,128)(2,1)}), bf16[4,160,960]{2,1,0:T(8,128)(2,1)}) %reduce-scatter.33.cloned.1.call-update) | async-done | bytes 1228816 | tf_op jit(solution)/shard_map/reduce_scatter | solution.py:131
  918.9 4.6 all-to-all-start.4
  923.5 58.0 %reduce-scatter.37.cloned.1.call-done = f32[160,2]{1,0:T(8,128)} async-done(((f32[2560,2]{1,0:T(8,128)}), f32[160,2]{1,0:T(8,128)}) %reduce-scatter.37.cloned.1.call-update) | async-done | bytes 1296
  982.5 4.9 psum.15
  987.4 47.1 %reduce-scatter.35.cloned.1.call-done = bf16[4,160,960]{2,1,0:T(8,128)(2,1)} async-done(((bf16[16,160,960]{2,1,0:T(8,128)(2,1)}), bf16[4,160,960]{2,1,0:T(8,128)(2,1)}) %reduce-scatter.35.cloned.1.call-update) | async-done | bytes 1228816 | tf_op jit(solution)/shard_map/reduce_scatter | solution.py:131
  1034.5 4.8 all-to-all-start.5
  1039.9 35.7 %all-gather.18.cloned.1.call-done = f32[2,128,2560]{2,1,0:T(8,128)} async-done(((f32[2,64,2560]{2,1,0:T(8,128)}), f32[2,128,2560]{2,1,0:T(8,128)}) %all-gather.18.cloned.1.call-update) | async-done | bytes 2621456 | tf_op jit(solution)/shard_map/all_gather | solution.py:281
  1075.6 3.4 fusion.83
  1079.0 64.6 %reduce-scatter.27.cloned.1.call-done = bf16[160,512]{1,0:T(8,128)(2,1)} async-done(((bf16[2560,512]{1,0:T(8,128)(2,1)}), bf16[160,512]{1,0:T(8,128)(2,1)}) %reduce-scatter.27.cloned.1.call-update) | async-done | bytes 163856 | tf_op jit(solution)/shard_map/reduce_scatter | solution.py:120
  1149.2 4.2 reshape.278
  1153.8 3.2 copy.253
  1156.9 4.4 reshape.279
  1166.2 4.5 reshape.280
  1170.8 8.5 multiply_subtract_fusion.2
  1180.4 4.5 multiply_subtract_fusion.1
  1186.9 4.3 multiply_subtract_fusion
  1191.2 42.0 %reduce-scatter.25.cloned.1.call-done = bf16[160,1280]{1,0:T(8,128)(2,1)} async-done(((bf16[2560,1280]{1,0:T(8,128)(2,1)}), bf16[160,1280]{1,0:T(8,128)(2,1)}) %reduce-scatter.25.cloned.1.call-update) | async-done | bytes 409616 | tf_op jit(solution)/shard_map/reduce_scatter | solution.py:120
  1236.4 86.6 %reduce-scatter.29.cloned.1.call-done = bf16[160,1280]{1,0:T(8,128)(2,1)} async-done(((bf16[2560,1280]{1,0:T(8,128)(2,1)}), bf16[160,1280]{1,0:T(8,128)(2,1)}) %reduce-scatter.29.cloned.1.call-update) | async-done | bytes 409616 | tf_op jit(solution)/shard_map/reduce_scatter | solution.py:120
  1323.0 3.4 multiply_subtract_fusion.3
  (271 shorter events, 101.7 us)
Async XLA Ops:
  8.0 17.0 %copy-start.24 = (f32[160,512]{1,0:T(8,128)S(1)}, f32[160,512]{1,0:T(8,128)}, u32[]{:S(2)}) copy-start(f32[160,512]{1,0:T(8,128)} %param.34) | copy-start | bytes 983044
  8.1 18.7 %copy-start.10 = (f32[1280,160]{0,1:T(8,128)S(1)}, f32[1280,160]{0,1:T(8,128)}, u32[]{:S(2)}) copy-start(f32[1280,160]{0,1:T(8,128)} %param.35) | copy-start | bytes 2457604
  8.1 19.2 %copy-start.51 = (f32[160]{0:T(256)S(1)}, f32[160]{0:T(256)}, u32[]{:S(2)}) copy-start(f32[160]{0:T(256)} %param.36) | copy-start | bytes 1924
  8.1 19.2 %copy-start.53 = (f32[160]{0:T(256)S(1)}, f32[160]{0:T(256)}, u32[]{:S(2)}) copy-start(f32[160]{0:T(256)} %param.32) | copy-start | bytes 1924
  8.1 433.6 %reduce-scatter.15.cloned.1.call-start = ((), (), s32[]{:S(2)}) async-start(), calls=%async_computation.18 | async-start | bytes 983040 | tf_op jit(solution)/shard_map/reduce_scatter | solution.py:214
  9.4 12.6 collective-permute-start.4
  22.2 81.9 %copy-start = (f32[1,128,2560]{2,1,0:T(8,128)S(1)}, f32[1,128,2560]{2,1,0:T(8,128)}, u32[]{:S(2)}) copy-start(f32[1,128,2560]{2,1,0:T(8,128)} %param.28) | copy-start | bytes 3932164
  22.2 38.0 %collective-permute-start.5 = (bf16[320,1280]{1,0:T(8,128)(2,1)S(1)}, bf16[320,1280]{1,0:T(8,128)(2,1)}, u32[]{:S(2)}, u32[]{:S(2)}) collective-permute-start(bf16[320,1280]{1,0:T(8,128)(2,1)S(1)} %maximum_select_fusion.11), channel_id=1, source_target_pairs={{0,4},{2,6},{4,0},{6,2},{8,12},{10,14},{12,8},{14,10},{16,20},{18,... | collective-permute-start | bytes 2457608 | tf_op jit(solution)/shard_map/ppermute | solution.py:25
  25.1 80.7 %collective-permute-start = (bf16[160,512]{1,0:T(8,128)(2,1)S(1)}, bf16[160,512]{1,0:T(8,128)(2,1)}, u32[]{:S(2)}, u32[]{:S(2)}) collective-permute-start(bf16[160,512]{1,0:T(8,128)(2,1)S(1)} %convert_element_type.181), channel_id=1, source_target_pairs={{0,2},{2,0},{4,6},{6,4},{8,10},{10,8},{12,14},{14,12},{16,18},{18,... | collective-permute-start | bytes 491528 | tf_op jit(solution)/shard_map/ppermute | solution.py:25
  26.8 81.3 %collective-permute-start.8 = (bf16[160,1280]{1,0:T(8,128)(2,1)S(1)}, bf16[160,1280]{1,0:T(8,128)(2,1)}, u32[]{:S(2)}, u32[]{:S(2)}) collective-permute-start(bf16[160,1280]{1,0:T(8,128)(2,1)S(1)} %convert_bitcast_fusion.5), channel_id=1, source_target_pairs={{0,2},{2,0},{4,6},{6,4},{8,10},{10,8},{12,14},{14,12},{16,18},{18,... | collective-permute-start | bytes 1228808 | tf_op jit(solution)/shard_map/ppermute | solution.py:25
  62.6 76.2 %collective-permute-start.6 = (bf16[640,1280]{1,0:T(8,128)(2,1)S(1)}, bf16[640,1280]{1,0:T(8,128)(2,1)}, u32[]{:S(2)}, u32[]{:S(2)}) collective-permute-start(bf16[640,1280]{1,0:T(8,128)(2,1)S(1)} %maximum_select_fusion.5), channel_id=1, source_target_pairs={{0,8},{2,10},{4,12},{6,14},{8,0},{10,2},{12,4},{14,6},{16,24},{18,... | collective-permute-start | bytes 4915208 | tf_op jit(solution)/shard_map/ppermute | solution.py:25
  105.8 180.1 %copy-start.43 = (f32[128]{0:T(128)}, f32[128]{0:T(128)S(1)}, u32[]{:S(2)}) copy-start(f32[128]{0:T(128)S(1)} %add_rsqrt_fusion.1) | copy-start | bytes 1540
  106.9 31.7 %collective-permute-start.1 = (bf16[320,512]{1,0:T(8,128)(2,1)S(1)}, bf16[320,512]{1,0:T(8,128)(2,1)S(1)}, u32[]{:S(2)}, u32[]{:S(2)}) collective-permute-start(bf16[320,512]{1,0:T(8,128)(2,1)S(1)} %maximum_select_fusion.18), channel_id=1, source_target_pairs={{0,4},{2,6},{4,0},{6,2},{8,12},{10,14},{12,8},{14,10},{16,20},{18,... | collective-permute-start | bytes 983048 | tf_op jit(solution)/shard_map/ppermute | solution.py:25
  108.0 637.9 %copy-start.36 = (f32[2560]{0:T(1024)}, f32[2560]{0:T(1024)S(1)}, u32[]{:S(2)}) copy-start(f32[2560]{0:T(1024)S(1)} %get-tuple-element.38) | copy-start | bytes 30724
  110.3 45.8 %collective-permute-start.9 = (bf16[320,1280]{1,0:T(8,128)(2,1)}, bf16[320,1280]{1,0:T(8,128)(2,1)}, u32[]{:S(2)}, u32[]{:S(2)}) collective-permute-start(bf16[320,1280]{1,0:T(8,128)(2,1)} %maximum_select_fusion.12), channel_id=1, source_target_pairs={{0,4},{2,6},{4,0},{6,2},{8,12},{10,14},{12,8},{14,10},{16,20},{18,... | collective-permute-start | bytes 2457608 | tf_op jit(solution)/shard_map/ppermute | solution.py:25
  138.8 5.1 collective-permute-start.2
  142.4 16.0 %copy-start.61 = (s32[1,128]{1,0:T(1,128)S(1)}, s32[1,128]{1,0:T(1,128)}, u32[]{:S(2)}) copy-start(s32[1,128]{1,0:T(1,128)} %param.31) | copy-start | bytes 1540
  142.4 124.3 %collective-permute-start.7 = (bf16[1280,1280]{1,0:T(8,128)(2,1)}, bf16[1280,1280]{1,0:T(8,128)(2,1)}, u32[]{:S(2)}, u32[]{:S(2)}) collective-permute-start(bf16[1280,1280]{1,0:T(8,128)(2,1)} %maximum_select_fusion.2), channel_id=1, source_target_pairs={{0,16},{2,18},{4,20},{6,22},{8,24},{10,26},{12,28},{14,30},{16,0},... | collective-permute-start | bytes 9830408 | tf_op jit(solution)/shard_map/ppermute | solution.py:25
  145.4 98.7 %collective-permute-start.3 = (bf16[1280,512]{1,0:T(8,128)(2,1)}, bf16[1280,512]{1,0:T(8,128)(2,1)}, u32[]{:S(2)}, u32[]{:S(2)}) collective-permute-start(bf16[1280,512]{1,0:T(8,128)(2,1)} %maximum_select_fusion.7), channel_id=1, source_target_pairs={{0,16},{2,18},{4,20},{6,22},{8,24},{10,26},{12,28},{14,30},{16,0},... | collective-permute-start | bytes 3932168 | tf_op jit(solution)/shard_map/ppermute | solution.py:25
  146.0 101.3 %copy-start.47 = (f32[128]{0:T(128)}, f32[128]{0:T(128)S(1)}, u32[]{:S(2)}) copy-start(f32[128]{0:T(128)S(1)} %multiply_power_fusion) | copy-start | bytes 1540
  158.4 89.3 %collective-permute-start.10 = (bf16[640,1280]{1,0:T(8,128)(2,1)S(1)}, bf16[640,1280]{1,0:T(8,128)(2,1)S(1)}, u32[]{:S(2)}, u32[]{:S(2)}) collective-permute-start(bf16[640,1280]{1,0:T(8,128)(2,1)S(1)} %maximum_select_fusion.6), channel_id=1, source_target_pairs={{0,8},{2,10},{4,12},{6,14},{8,0},{10,2},{12,4},{14,6},{16,24},{18,... | collective-permute-start | bytes 4915208 | tf_op jit(solution)/shard_map/ppermute | solution.py:25
  158.5 88.8 %copy-start.48 = (f32[128]{0:T(128)}, f32[128]{0:T(128)S(1)}, u32[]{:S(2)}) copy-start(f32[128]{0:T(128)S(1)} %convert_bitcast_fusion.6) | copy-start | bytes 1540
  249.8 72.8 %collective-permute-start.11 = (bf16[1280,1280]{1,0:T(8,128)(2,1)}, bf16[1280,1280]{1,0:T(8,128)(2,1)}, u32[]{:S(2)}, u32[]{:S(2)}) collective-permute-start(bf16[1280,1280]{1,0:T(8,128)(2,1)} %maximum_select_fusion.3), channel_id=1, source_target_pairs={{0,16},{2,18},{4,20},{6,22},{8,24},{10,26},{12,28},{14,30},{16,0},... | collective-permute-start | bytes 9830408 | tf_op jit(solution)/shard_map/ppermute | solution.py:25
  266.7 25.1 %copy-start.18 = (bf16[512,512]{1,0:T(8,128)(2,1)}, bf16[512,512]{1,0:T(8,128)(2,1)S(1)}, u32[]{:S(2)}) copy-start(bf16[512,512]{1,0:T(8,128)(2,1)S(1)} %all_gather.31) | copy-start | bytes 1572868
  293.0 29.5 %copy-start.20 = (bf16[256,5,128]{2,0,1:T(8,128)(2,1)}, bf16[256,5,128]{2,0,1:T(8,128)(2,1)S(1)}, u32[]{:S(2)}) copy-start(bf16[256,5,128]{2,0,1:T(8,128)(2,1)S(1)} %convolution_convert_fusion.10) | copy-start | bytes 983044
  329.8 156.2 %all-gather.16.cloned.1.call-start = ((), (), s32[]{:S(2)}) async-start(), calls=%async_computation.24 | async-start | bytes 2949120 | tf_op jit(solution)/shard_map/all_gather | solution.py:110
  331.7 154.3 %all-gather.14.cloned.1.call-start = ((), (), s32[]{:S(2)}) async-start(), calls=%async_computation.22 | async-start | bytes 6553600 | tf_op jit(solution)/shard_map/all_gather | solution.py:105
  401.2 92.1 %all-gather.10.cloned.1.call-start = ((), (), s32[]{:S(2)}) async-start(), calls=%async_computation.20 | async-start | bytes 6553600 | tf_op jit(solution)/shard_map/all_gather | solution.py:105
  441.6 102.2 %all-gather.8.cloned.1.call-start = ((), (), s32[]{:S(2)}) async-start(), calls=%async_computation.19 | async-start | bytes 2949120 | tf_op jit(solution)/shard_map/all_gather | solution.py:110
  443.7 140.5 %all-gather.12.cloned.1.call-start = ((), (), s32[]{:S(2)}) async-start(), calls=%async_computation.21 | async-start | bytes 6553600 | tf_op jit(solution)/shard_map/all_gather | solution.py:105
  485.7 187.0 %reduce-scatter.19.cloned.1.call-start = ((), (), s32[]{:S(2)}) async-start(), calls=%async_computation.25 | async-start | bytes 2949120 | tf_op jit(solution)/shard_map/reduce_scatter | solution.py:114
  584.3 9.6 copy-start.59
  601.5 144.5 %reduce-scatter.17.cloned.1.call-start = ((), (), s32[]{:S(2)}) async-start(), calls=%async_computation.23 | async-start | bytes 2949120 | tf_op jit(solution)/shard_map/reduce_scatter | solution.py:114
  608.8 205.8 %reduce-scatter.23.cloned.1.call-start = ((), (), s32[]{:S(2)}) async-start(), calls=%async_computation.27 | async-start | bytes 655360 | tf_op jit(solution)/shard_map/reduce_scatter | solution.py:247
  674.0 90.7 %copy-start.49 = (f32[64]{0:T(128)}, f32[64]{0:T(128)S(1)}, u32[]{:S(2)}) copy-start(f32[64]{0:T(128)S(1)} %broadcast_multiply_fusion.1) | copy-start | bytes 772
  772.6 57.0 %reduce-scatter.21.cloned.1.call-start = ((), (), s32[]{:S(2)}) async-start(), calls=%async_computation.26 | async-start | bytes 983040 | tf_op jit(solution)/shard_map/reduce_scatter | solution.py:260
  783.6 81.5 %reduce-scatter.31.cloned.1.call-start = ((), (), s32[]{:S(2)}) async-start(), calls=%async_computation.32 | async-start | bytes 6553600 | tf_op jit(solution)/shard_map/reduce_scatter | solution.py:131
  798.5 120.4 %reduce-scatter.33.cloned.1.call-start = ((), (), s32[]{:S(2)}) async-start(), calls=%async_computation.33 | async-start | bytes 6553600 | tf_op jit(solution)/shard_map/reduce_scatter | solution.py:131
  813.9 167.6 %reduce-scatter.37.cloned.1.call-start = ((), (), s32[]{:S(2)}) async-start(), calls=%async_computation.35 | async-start | bytes 1392640
  835.9 198.5 %reduce-scatter.35.cloned.1.call-start = ((), (), s32[]{:S(2)}) async-start(), calls=%async_computation.34 | async-start | bytes 6553600 | tf_op jit(solution)/shard_map/reduce_scatter | solution.py:131
  850.9 224.7 %all-gather.18.cloned.1.call-start = ((), (), s32[]{:S(2)}) async-start(), calls=%async_computation.28 | async-start | bytes 3932160 | tf_op jit(solution)/shard_map/all_gather | solution.py:281
  854.6 289.0 %reduce-scatter.27.cloned.1.call-start = ((), (), s32[]{:S(2)}) async-start(), calls=%async_computation.30 | async-start | bytes 2785280 | tf_op jit(solution)/shard_map/reduce_scatter | solution.py:120
  857.2 376.1 %reduce-scatter.25.cloned.1.call-start = ((), (), s32[]{:S(2)}) async-start(), calls=%async_computation.29 | async-start | bytes 6963200 | tf_op jit(solution)/shard_map/reduce_scatter | solution.py:120
  865.2 53.8 %all-to-all-start.3 = ((bf16[4,160,960]{2,1,0:T(8,128)(2,1)}), bf16[4,160,960]{2,1,0:T(8,128)(2,1)S(1)}, u32[]{:S(2)}, u32[]{:S(2)}) async-start(bf16[4,160,960]{2,1,0:T(8,128)(2,1)} %reduce-scatter.31.cloned.1.call-done), calls=%async_computation.12 | async-start | bytes 2621440 | tf_op jit(solution)/shard_map/all_to_all | solution.py:132
  869.8 453.2 %reduce-scatter.29.cloned.1.call-start = ((), (), s32[]{:S(2)}) async-start(), calls=%async_computation.31 | async-start | bytes 6963200 | tf_op jit(solution)/shard_map/reduce_scatter | solution.py:120
  874.8 164.5 %copy-start.52 = (f32[160]{0:T(256)S(1)}, f32[160]{0:T(256)}, u32[]{:S(2)}) copy-start(f32[160]{0:T(256)} %param.36) | copy-start | bytes 1924
  874.8 164.5 %copy-start.54 = (f32[160]{0:T(256)S(1)}, f32[160]{0:T(256)}, u32[]{:S(2)}) copy-start(f32[160]{0:T(256)} %param.32) | copy-start | bytes 1924
  874.8 164.5 %copy-start.55 = (f32[160]{0:T(256)S(1)}, f32[160]{0:T(256)}, u32[]{:S(2)}) copy-start(f32[160]{0:T(256)} %param.44) | copy-start | bytes 1924
  874.8 164.5 %copy-start.56 = (f32[160]{0:T(256)S(1)}, f32[160]{0:T(256)}, u32[]{:S(2)}) copy-start(f32[160]{0:T(256)} %param.52) | copy-start | bytes 1924
  874.8 164.5 %copy-start.57 = (f32[160]{0:T(256)S(1)}, f32[160]{0:T(256)}, u32[]{:S(2)}) copy-start(f32[160]{0:T(256)} %param.48) | copy-start | bytes 1924
  874.8 164.5 %copy-start.58 = (f32[160]{0:T(256)S(1)}, f32[160]{0:T(256)}, u32[]{:S(2)}) copy-start(f32[160]{0:T(256)} %param.40) | copy-start | bytes 1924
  918.9 115.5 %all-to-all-start.4 = ((bf16[4,160,960]{2,1,0:T(8,128)(2,1)}), bf16[4,160,960]{2,1,0:T(8,128)(2,1)S(1)}, u32[]{:S(2)}, u32[]{:S(2)}) async-start(bf16[4,160,960]{2,1,0:T(8,128)(2,1)} %reduce-scatter.33.cloned.1.call-done), calls=%async_computation.14 | async-start | bytes 2621440 | tf_op jit(solution)/shard_map/all_to_all | solution.py:132
  987.4 91.6 %copy-start.45 = (f32[1,160]{1,0:T(1,128)}, f32[1,160]{1,0:T(1,128)S(1)}, u32[]{:S(2)}) copy-start(f32[1,160]{1,0:T(1,128)S(1)} %get-tuple-element.84) | copy-start | bytes 1924
  987.4 91.6 %copy-start.46 = (f32[1,160]{1,0:T(1,128)}, f32[1,160]{1,0:T(1,128)S(1)}, u32[]{:S(2)}) copy-start(f32[1,160]{1,0:T(1,128)S(1)} %get-tuple-element.85) | copy-start | bytes 1924
  1034.5 126.9 %all-to-all-start.5 = ((bf16[4,160,960]{2,1,0:T(8,128)(2,1)}), bf16[4,160,960]{2,1,0:T(8,128)(2,1)}, u32[]{:S(2)}, u32[]{:S(2)}) async-start(bf16[4,160,960]{2,1,0:T(8,128)(2,1)} %reduce-scatter.35.cloned.1.call-done), calls=%async_computation.16 | async-start | bytes 2621440 | tf_op jit(solution)/shard_map/all_to_all | solution.py:132
  1039.9 103.7 %copy-start.25 = (f32[160,512]{1,0:T(8,128)S(1)}, f32[160,512]{1,0:T(8,128)}, u32[]{:S(2)}) copy-start(f32[160,512]{1,0:T(8,128)} %param.34) | copy-start | bytes 983044
  1039.9 103.7 %copy-start.35 = (f32[160,512]{1,0:T(8,128)S(1)}, f32[160,512]{1,0:T(8,128)}, u32[]{:S(2)}) copy-start(f32[160,512]{1,0:T(8,128)} %param.42) | copy-start | bytes 983044
  1170.7 8.6 copy-start.1
  1170.7 8.6 copy-start.3
  1170.7 8.6 copy-start.14
  1170.8 9.6 copy-start.15
  1186.9 46.3 %copy-start.9 = (f32[160,1280]{1,0:T(8,128)S(1)}, f32[160,1280]{1,0:T(8,128)}, u32[]{:S(2)}) copy-start(f32[160,1280]{1,0:T(8,128)} %param.33) | copy-start | bytes 2457604
  1186.9 46.3 %copy-start.31 = (f32[160,1280]{1,0:T(8,128)S(1)}, f32[160,1280]{1,0:T(8,128)}, u32[]{:S(2)}) copy-start(f32[160,1280]{1,0:T(8,128)} %param.41) | copy-start | bytes 2457604
  1191.2 131.8 %copy-start.11 = (f32[1280,160]{0,1:T(8,128)S(1)}, f32[1280,160]{0,1:T(8,128)}, u32[]{:S(2)}) copy-start(f32[1280,160]{0,1:T(8,128)} %param.35) | copy-start | bytes 2457604
  (33 other events, 98.9 us)
Sparse Core Ops, SparseCore 0:
  329.9 15.6 reduce-scatter.14
  772.7 21.3 reduce-scatter.22
  797.0 14.3 reduce-scatter.20
  813.8 51.3 reduce-scatter.30
  867.5 51.3 reduce-scatter.32
  923.0 58.4 reduce-scatter.36
  984.0 50.3 reduce-scatter.34
  1036.6 38.9 all-gather.17
  1079.4 64.2 reduce-scatter.26
  1147.4 85.7 reduce-scatter.24
  1237.2 85.7 reduce-scatter.28
Sparse Core Ops, SparseCore 1:
  333.0 71.1 all-gather.15
  405.6 39.2 all-gather.13
  446.2 40.2 all-gather.9
  489.3 54.4 all-gather.7
  545.4 38.8 all-gather.11
  601.6 71.1 reduce-scatter.18
  676.1 69.8 reduce-scatter.16
